TPU v7x, 32 devices: a whole 2x2x4 slice. The times are simulated.
32 devices in a mesh: snap: 4 (over z), param: 8 (over y, x, core).
Axes of the slice: x: 2, y: 2, z: 4, core: 2. Of those that a mesh axis runs over, the one named last changes fastest.
Arguments:
- snapshots: bfloat16 [256, 512, 1024], P('snap', 'param'), as said below
- coeffs: float32 [16, 256], P(None, 'snap'), may hold values from -0.375 to 0.375
Outputs:
- averages: float32 [16, 512, 1024], P(None, 'param', 'snap')
- width_norms: float32 [16], replicated
Inputs may be any that keep to these rules, and one draw needn't show every extreme that they name: `snapshots`: stored snapshot weights, finite.
All inputs are finite; a program needn't handle non-finite values.
Results may differ from a plain program's by a relative error of at most 0.0003.
Values may be sent and summed in bfloat16 or wider, within the bound.
A program may use at most 64 MiB of HBM per device.

v0:
```python
import functools

import jax
import jax.numpy as jnp
from jax import lax
from jax.experimental import pallas as pl
from jax.experimental.pallas import tpu as pltpu
from jax.sharding import PartitionSpec as P

MESH = pl.DeviceIdType.MESH
GROUP = 16
LAG = 3
POWER = 15
AHEAD = 4
TOP = 2.0**8.375


def encode(value):
    largest = jnp.max(jnp.max(jnp.abs(value), axis=0), axis=0, keepdims=True)
    largest = jnp.maximum(largest, 1e-30)
    x = value * (TOP / largest)[None]
    x2 = x * x
    x4 = x2 * x2
    x8 = x4 * x4
    return ((x8 * x4) * (x2 * x)).astype(jnp.bfloat16), largest * (1.0 / TOP)


def decode(code, scale):
    y = code.astype(jnp.float32)
    size = jnp.exp2(jnp.log2(jnp.maximum(jnp.abs(y), 1e-38)) * (1.0 / POWER)) * scale[None]
    return jnp.where(y > 0.0, size, jnp.where(y < 0.0, -size, 0.0))


def each(size, body):
    if size <= 8:
        for k in range(size):
            body(k)
    else:
        pl.loop(0, size)(body)


def kernel(
    n, peers, entries, coeffs, stored, averages, norms,
    spread, tiles, part, out_code, out_scale, in_code, in_scale, squares, lines,
    load_sem, send_sem, send_scale_sem, recv_sem, recv_scale_sem,
    line_send, line_recv, known,
):
    z = lax.axis_index("snap")
    me = lax.axis_index("param")
    widths, count = coeffs.shape
    keep = stored.shape[2] // n
    groups = stored.shape[1] // GROUP
    steps = (n - 1) * groups
    lag = min(LAG, groups - 1)
    low = z < n // 2

    def load(i):
        q, t = i // groups, lax.rem(i, groups)
        d = jnp.where(low, n - 1 - q, q)
        return pltpu.make_async_copy(
            stored.at[:, pl.ds(pl.multiple_of(t * GROUP, GROUP), GROUP), pl.ds(pl.multiple_of(d * keep, keep), keep)],
            tiles.at[i],
            load_sem.at[i],
        )

    load(0).start()
    barrier = pltpu.get_barrier_semaphore()

    def greet(axis, mine):
        def body(k):
            @pl.when(k != mine)
            def _():
                pl.semaphore_signal(barrier, inc=1, device_id={axis: k}, device_id_type=MESH)

        return body

    each(n, greet("snap", z))
    each(peers, greet("param", me))
    for i in range(1, min(AHEAD, n * groups)):
        load(i).start()

    whole = coeffs[...]
    high = whole.astype(jnp.bfloat16)
    rest = (whole - high.astype(jnp.float32)).astype(jnp.bfloat16)
    both = jnp.concatenate([high, rest], axis=0)
    tall, wide = spread.shape
    row = lax.broadcasted_iota(jnp.int32, (tall, 2 * widths), 0)
    col = lax.broadcasted_iota(jnp.int32, (tall, 2 * widths), 1)
    pick = jnp.where(row // GROUP == col, 1.0, 0.0).astype(jnp.bfloat16)
    row = lax.broadcasted_iota(jnp.int32, (count, wide), 0)
    col = lax.broadcasted_iota(jnp.int32, (count, wide), 1)
    repeat = jnp.where(col // GROUP == row, 1.0, 0.0).astype(jnp.bfloat16)
    tall_rows = jnp.dot(pick, both, preferred_element_type=jnp.float32).astype(jnp.bfloat16)
    full = jnp.dot(tall_rows, repeat, preferred_element_type=jnp.float32)
    row = lax.broadcasted_iota(jnp.int32, (GROUP, wide), 0)
    col = lax.broadcasted_iota(jnp.int32, (GROUP, wide), 1)
    same = (row == col % GROUP)[None]
    full = jnp.where(same, full.reshape(2 * widths, GROUP, wide), 0.0)
    spread[...] = full.reshape(tall, wide).astype(jnp.bfloat16)

    def copies(way, k, peer):
        code = pltpu.make_async_remote_copy(
            src_ref=out_code.at[way, k], dst_ref=in_code.at[way, k],
            send_sem=send_sem.at[way, k], recv_sem=recv_sem.at[way, k],
            device_id={"snap": peer}, device_id_type=MESH,
        )
        scale = pltpu.make_async_remote_copy(
            src_ref=out_scale.at[way, k], dst_ref=in_scale.at[way, k],
            send_sem=send_scale_sem.at[way, k], recv_sem=recv_scale_sem.at[way, k],
            device_id={"snap": peer}, device_id_type=MESH,
        )
        return scale, code

    def send(way, k, peer, value):
        code, scale = encode(value)
        out_code[way, k] = code
        out_scale[way, k] = scale
        for copy in copies(way, k, peer):
            copy.start()

    half = widths * GROUP

    @pl.loop(0, n * groups)
    def _(i):
        q, t = i // groups, lax.rem(i, groups)
        d = jnp.where(low, n - 1 - q, q)
        load(i).wait()

        @pl.when(i + AHEAD < n * groups)
        def _():
            load(i + AHEAD).start()

        both_parts = jnp.dot(
            spread[...], tiles[i].reshape(count * GROUP, keep), preferred_element_type=jnp.float32
        )
        value = (both_parts[:half] + both_parts[half:]).reshape(widths, GROUP, keep)
        part[d, t] = value

        @pl.when(i == 0)
        def _():
            pl.semaphore_wait(barrier, n - 1 + peers - 1)

        @pl.when(jnp.logical_and(jnp.logical_or(z == 0, z == n - 1), d != z))
        def _():
            way = jnp.where(z == 0, 0, 1)
            peer = jnp.where(z == 0, 1, n - 2)
            send(way, i, peer, value)

    def inform(k):
        @pl.when(k != me)
        def _():
            pl.semaphore_signal(known, inc=1, device_id={"param": k}, device_id_type=MESH)

    each(peers, inform)

    last = jnp.where(jnp.logical_or(jnp.logical_and(z > 0, 2 * z < n - 1), z == n - 1), 0, 1)

    def pass_on(way, k, d, peer):
        t = lax.rem(k, groups)
        for copy in copies(way, k, peer):
            copy.wait_recv()
        value = part[d, t] + decode(in_code[way, k], in_scale[way, k])

        @pl.when(d == z)
        def _():
            @pl.when(way != last)
            def _():
                part[d, t] = value

            @pl.when(way == last)
            def _():
                averages[:, pl.ds(pl.multiple_of(t * GROUP, GROUP), GROUP), :] = value
                squares[t] = jnp.sum(value * value, axis=1)

        @pl.when(d != z)
        def _():
            send(way, k, peer, value)

    @pl.loop(0, steps)
    def _(j):
        up = j - lag * (z - 1)

        @pl.when(jnp.logical_and(z > 0, jnp.logical_and(up >= 0, up < (n - z) * groups)))
        def _():
            pass_on(0, up, n - 1 - up // groups, jnp.where(z == n - 1, z - 1, z + 1))

        down = j - lag * (n - 2 - z)

        @pl.when(jnp.logical_and(z < n - 1, jnp.logical_and(down >= 0, down < (z + 1) * groups)))
        def _():
            pass_on(1, down, down // groups, jnp.where(z == 0, z + 1, z - 1))

    sums = jnp.sum(jnp.sum(squares[...], axis=0), axis=1, keepdims=True)
    lanes = norms.shape[1]
    row = lax.broadcasted_iota(jnp.int32, (widths, lanes), 0)
    col = lax.broadcasted_iota(jnp.int32, (widths, lanes), 1)
    line = jnp.sum(jnp.where(row == col, sums, 0.0), axis=0, keepdims=True)

    own = z * peers + me
    lines[own] = line
    pl.semaphore_wait(known, peers - 1)

    def others(act):
        for p in range(n):
            def body(k, p=p):
                @pl.when(jnp.logical_or(p != z, k != me))
                def _():
                    act(p, k)

            each(peers, body)

    def line_copy(p, k, slot):
        return pltpu.make_async_remote_copy(
            src_ref=lines.at[slot], dst_ref=lines.at[slot],
            send_sem=line_send.at[p * peers + k], recv_sem=line_recv.at[slot],
            device_id={"snap": p, "param": k}, device_id_type=MESH,
        )

    others(lambda p, k: line_copy(p, k, own).start())

    @pl.loop(0, steps)
    def _(k):
        @pl.when(k < (n - 1 - z) * groups)
        def _():
            for copy in copies(0, k, jnp.where(z == n - 1, z - 1, z + 1)):
                copy.wait_send()

        @pl.when(k < z * groups)
        def _():
            for copy in copies(1, k, jnp.where(z == 0, z + 1, z - 1)):
                copy.wait_send()

    others(lambda p, k: line_copy(p, k, own).wait_send())
    others(lambda p, k: line_copy(p, k, p * peers + k).wait_recv())
    norms[...] = jnp.sqrt(jnp.sum(lines[...], axis=0) / jnp.float32(entries))


def on_device(n, peers, snapshots, coeffs):
    count, height, cols = snapshots.shape
    widths = coeffs.shape[0]
    keep = cols // n
    groups = height // GROUP
    steps = (n - 1) * groups
    entries = height * cols * peers
    dma = pltpu.SemaphoreType.DMA
    averages, norms = pl.pallas_call(
        functools.partial(kernel, n, peers, entries),
        out_shape=(
            jax.ShapeDtypeStruct((widths, height, keep), jnp.float32),
            jax.ShapeDtypeStruct((1, 128), jnp.float32),
        ),
        in_specs=[pl.BlockSpec(memory_space=pltpu.VMEM), pl.BlockSpec(memory_space=pl.ANY)],
        out_specs=(pl.BlockSpec(memory_space=pltpu.VMEM), pl.BlockSpec(memory_space=pltpu.VMEM)),
        scratch_shapes=[
            pltpu.VMEM((2 * widths * GROUP, count * GROUP), jnp.bfloat16),
            pltpu.VMEM((n * groups, count, GROUP, keep), jnp.bfloat16),
            pltpu.VMEM((n, groups, widths, GROUP, keep), jnp.float32),
            pltpu.VMEM((2, steps, widths, GROUP, keep), jnp.bfloat16),
            pltpu.VMEM((2, steps, 1, keep), jnp.float32),
            pltpu.VMEM((2, steps, widths, GROUP, keep), jnp.bfloat16),
            pltpu.VMEM((2, steps, 1, keep), jnp.float32),
            pltpu.VMEM((groups, widths, keep), jnp.float32),
            pltpu.VMEM((n * peers, 1, 128), jnp.float32),
            dma((n * groups,)),
            dma((2, steps)), dma((2, steps)), dma((2, steps)), dma((2, steps)),
            dma((n * peers,)), dma((n * peers,)), pltpu.SemaphoreType.REGULAR,
        ],
        compiler_params=pltpu.CompilerParams(
            collective_id=0, has_side_effects=True, vmem_limit_bytes=48 * 1024 * 1024
        ),
        name="reconstruct",
    )(coeffs, snapshots)
    return averages, norms[0, :widths]


def solution(mesh):
    in_specs = (P("snap", "param", None), P(None, "snap"))
    out_specs = (P(None, "param", "snap"), P())
    body = functools.partial(on_device, mesh.shape["snap"], mesh.shape["param"])
    return jax.shard_map(body, mesh=mesh, in_specs=in_specs, out_specs=out_specs, check_vma=False)
```

profile of v0, /device:TPU:0, one launch (start us, length us, event | category | flops | bytes accessed | tf_op | source)
XLA Modules:
  0.0 50.3 jit_solution(13667216421776954838)
XLA Ops:
  0.6 0.0 copy-start
  0.6 0.7 %copy-done = f32[16,64]{1,0:T(8,128)S(1)} copy-done((f32[16,64]{1,0:T(8,128)S(1)}, f32[16,64]{1,0:T(8,128)}, u32[]{:S(2)}) %copy-start) | copy-done | bytes 4120
  1.3 47.4 %reconstruct.1 = (f32[16,64,256]{2,1,0:T(8,128)S(1)}, f32[1,128]{1,0:T(1,128)S(1)}) custom-call(f32[16,64]{1,0:T(8,128)S(1)} %copy-done, bf16[64,64,1024]{2,1,0:T(8,128)(2,1)} %stored.1), custom_call_target="tpu_custom_call" | custom-call | tf_op jit(solution)/shard_map/reconstruct/pallas_call | solution.py:246
  48.8 0.5 %slice_bitcast_fusion = f32[16]{0:T(128)} fusion(f32[1,128]{1,0:T(1,128)S(1)} %get-tuple-element.5), kind=kLoop, calls=%fused_computation | loop fusion | bytes 128 | tf_op jit(solution)/shard_map/squeeze | solution.py:273
  49.3 1.0 %copy.5 = f32[16,64,256]{2,1,0:T(8,128)} copy(f32[16,64,256]{2,1,0:T(8,128)S(1)} %get-tuple-element.8) | data formatting | bytes 2097152
Async XLA Ops:
  0.6 0.7 %copy-start = (f32[16,64]{1,0:T(8,128)S(1)}, f32[16,64]{1,0:T(8,128)}, u32[]{:S(2)}) copy-start(f32[16,64]{1,0:T(8,128)} %coeffs.1) | copy-start | bytes 12292
where the time goes:
time: 50.4 us; the launch traced here: 50.3 us
  Pallas kernels  47.4 us (94%)
  local copies, waits for them, and re-layouts  2.17 us (4%)
  between operations  0.65 us (1%)
    pallas_call x1, Pallas kernels, on_device(): pl.pallas_call(functools.partial(kernel, n, peers, entries), out_shape=(j...  47.4 us
    unnamed x3, local copies, waits for them, and re-layouts  1.66 us

commit v1 on v0

v1 whole, which is shorter than its diff:
```python
import functools

import jax
import jax.numpy as jnp
from jax import lax
from jax.experimental import pallas as pl
from jax.experimental.pallas import tpu as pltpu
from jax.sharding import PartitionSpec as P

MESH = pl.DeviceIdType.MESH
GROUP = 16
WIDE = 128
LAG = 3
LATE = 5
POWER = 15
AHEAD = 6
TOP = 2.0**8.375


def encode(value):
    largest = jnp.max(jnp.max(jnp.abs(value), axis=0), axis=0, keepdims=True)
    largest = jnp.maximum(largest, 1e-30)
    x = value * (TOP / largest)[None]
    x2 = x * x
    x4 = x2 * x2
    x8 = x4 * x4
    return ((x8 * x4) * (x2 * x)).astype(jnp.bfloat16), largest * (1.0 / TOP)


def decode(code, scale):
    y = code.astype(jnp.float32)
    size = jnp.exp2(jnp.log2(jnp.maximum(jnp.abs(y), 1e-38)) * (1.0 / POWER)) * scale[None]
    return jnp.where(y > 0.0, size, jnp.where(y < 0.0, -size, 0.0))


def each(size, body):
    if size <= 8:
        for k in range(size):
            body(k)
    else:
        pl.loop(0, size)(body)


def kernel(
    n, peers, entries, coeffs, stored, averages, norms,
    weights, spread, tiles, part, out_code, out_scale, in_code, in_scale, squares, lines,
    coeff_sem, load_sem, send_sem, send_scale_sem, recv_sem, recv_scale_sem,
    line_send, line_recv, known, token_up, token_down, complete,
):
    z = lax.axis_index("snap")
    me = lax.axis_index("param")
    widths, count = coeffs.shape
    keep = stored.shape[2] // n
    cuts = keep // WIDE
    groups = stored.shape[1] // GROUP * cuts
    steps = (n - 1) * groups
    lag = min(LAG, groups - 1)
    late = max(0, min(LATE, groups - lag, (n - 3) * (groups - lag)))
    low = z < n // 2
    first, final = z == 0, z == n - 1
    end = jnp.logical_or(first, final)
    middle = jnp.logical_not(end)
    hub = middle if n > 2 else end

    def turned(d, s, last):
        return jnp.where(d == last, groups - 1 - s, s) if late > 0 else s

    def upwards(k):
        d = n - 1 - k // groups
        return d, turned(d, lax.rem(k, groups), n - 2)

    def downwards(k):
        d = k // groups
        return d, turned(d, lax.rem(k, groups), 1)

    def own(i):
        du, tu = upwards(i)
        dd, td = downwards(i)
        return jnp.where(low, du, dd), jnp.where(low, tu, td)

    def spot(t):
        return (
            pl.ds(pl.multiple_of(t // cuts * GROUP, GROUP), GROUP),
            pl.ds(pl.multiple_of(lax.rem(t, cuts) * WIDE, WIDE), WIDE),
        )

    def load(i):
        d, t = own(i)
        column = d * keep + lax.rem(t, cuts) * WIDE
        return pltpu.make_async_copy(
            stored.at[:, pl.ds(pl.multiple_of(t // cuts * GROUP, GROUP), GROUP), pl.ds(pl.multiple_of(column, WIDE), WIDE)],
            tiles.at[i],
            load_sem.at[i],
        )

    read = pltpu.make_async_copy(coeffs, weights, coeff_sem)
    read.start()
    load(0).start()
    barrier = pltpu.get_barrier_semaphore()

    @pl.when(z > 0)
    def _():
        pl.semaphore_signal(barrier, inc=1, device_id={"snap": z - 1}, device_id_type=MESH)

    @pl.when(z < n - 1)
    def _():
        pl.semaphore_signal(barrier, inc=1, device_id={"snap": z + 1}, device_id_type=MESH)

    for i in range(1, min(AHEAD, n * groups)):
        load(i).start()

    def to_peers(semaphore):
        def body(k):
            @pl.when(k != me)
            def _():
                pl.semaphore_signal(semaphore, inc=1, device_id={"param": k}, device_id_type=MESH)

        each(peers, body)

    @pl.when(hub)
    def _():
        to_peers(barrier)

    tall, wide = spread.shape
    row = lax.broadcasted_iota(jnp.int32, (count, wide), 0)
    col = lax.broadcasted_iota(jnp.int32, (count, wide), 1)
    repeat = jnp.where(col // GROUP == row, 1.0, 0.0).astype(jnp.bfloat16)
    row = lax.broadcasted_iota(jnp.int32, (GROUP, wide), 0)
    col = lax.broadcasted_iota(jnp.int32, (GROUP, wide), 1)
    same = (row == col % GROUP)[None]
    read.wait()
    whole = weights[...]
    high = whole.astype(jnp.bfloat16)
    rest = (whole - high.astype(jnp.float32)).astype(jnp.bfloat16)
    both = jnp.concatenate([high, rest], axis=0)
    full = jnp.dot(both, repeat, preferred_element_type=jnp.float32)
    full = jnp.where(same, full[:, None, :], 0.0)
    spread[...] = full.reshape(tall, wide).astype(jnp.bfloat16)
    squares[...] = jnp.zeros_like(squares)

    def copies(way, k, peer):
        code = pltpu.make_async_remote_copy(
            src_ref=out_code.at[way, k], dst_ref=in_code.at[way, k],
            send_sem=send_sem.at[way, k], recv_sem=recv_sem.at[way, k],
            device_id={"snap": peer}, device_id_type=MESH,
        )
        scale = pltpu.make_async_remote_copy(
            src_ref=out_scale.at[way, k], dst_ref=in_scale.at[way, k],
            send_sem=send_scale_sem.at[way, k], recv_sem=recv_scale_sem.at[way, k],
            device_id={"snap": peer}, device_id_type=MESH,
        )
        return scale, code

    def send(way, k, peer, value):
        code, scale = encode(value)
        out_code[way, k] = code
        out_scale[way, k] = scale
        for copy in copies(way, k, peer):
            copy.start()

    def arrived(way, k):
        for copy in copies(way, k, jnp.where(z == n - 1, z - 1, z + 1)):
            copy.wait_recv()
        return decode(in_code[way, k], in_scale[way, k])

    def count_squares(value):
        squares[...] += jnp.sum((value * value).reshape(widths, GROUP // 8, 8, WIDE), axis=1)

    half = widths * GROUP
    total = n * groups

    @pl.loop(0, total)
    def _(i):
        d, t = own(i)
        load(i).wait()

        @pl.when(i + AHEAD < total)
        def _():
            load(i + AHEAD).start()

        both_parts = jnp.dot(
            spread[...], tiles[i].reshape(count * GROUP, WIDE), preferred_element_type=jnp.float32
        )
        value = (both_parts[:half] + both_parts[half:]).reshape(widths, GROUP, WIDE)
        part[d, t] = value

        @pl.when(jnp.logical_and(i == 0, end))
        def _():
            pl.semaphore_wait(barrier, 1 if n > 2 else peers)

        @pl.when(jnp.logical_and(end, d != z))
        def _():
            send(jnp.where(first, 0, 1), i, jnp.where(first, 1, n - 2), value)

        @pl.when(jnp.logical_and(i == total // 4, middle))
        def _():
            pl.semaphore_wait(barrier, 2 + peers - 1)

        @pl.when(jnp.logical_and(i == total // 4, hub))
        def _():
            to_peers(known)

        @pl.when(jnp.logical_and(i == total // 2, hub))
        def _():
            pl.semaphore_wait(known, peers - 1)

        @pl.when(jnp.logical_and(i == total // 2, middle))
        def _():
            @pl.when(z > 1)
            def _():
                pl.semaphore_signal(token_down, inc=1, device_id={"snap": z - 1}, device_id_type=MESH)

            @pl.when(z < n - 2)
            def _():
                pl.semaphore_signal(token_up, inc=1, device_id={"snap": z + 1}, device_id_type=MESH)

    if n > 4:
        raise NotImplementedError

    @pl.when(middle)
    def _():
        @pl.when(z > 1)
        def _():
            pl.semaphore_wait(token_up, 1)

        @pl.when(z < n - 2)
        def _():
            pl.semaphore_wait(token_down, 1)

        @pl.when(z == 1)
        def _():
            pl.semaphore_signal(complete, inc=1, device_id={"snap": z - 1}, device_id_type=MESH)

        @pl.when(z == n - 2)
        def _():
            pl.semaphore_signal(complete, inc=1, device_id={"snap": z + 1}, device_id_type=MESH)

    def settle(t, value, counted):
        rows, columns = spot(t)
        averages[:, rows, columns] = value

        @pl.when(counted)
        def _():
            count_squares(value)

    def pass_on(j):
        up = j - lag * (z - 1)
        down = j - lag * (n - 2 - z)

        @pl.when(jnp.logical_and(up >= 0, up < (n - z) * groups))
        def _():
            d, t = upwards(up)
            value = part[d, t] + arrived(0, up)

            @pl.when(d == z)
            def _():
                s = jnp.where(z == 1, groups - 1 - t, t) if late > 0 else t
                second = z * groups + s + lag * (n - 2 - z) < j

                @pl.when(second)
                def _():
                    settle(t, value, jnp.logical_or(z != 1, t < groups - late))

                @pl.when(jnp.logical_not(second))
                def _():
                    part[d, t] = value

            extra = jnp.logical_and(z == n - 2, up < groups + late) if late > 0 else False

            @pl.when(jnp.logical_or(d != z, extra))
            def _():
                send(0, up, z + 1, value)

        @pl.when(jnp.logical_and(down >= 0, down < (z + 1) * groups))
        def _():
            d, t = downwards(down)
            value = part[d, t] + arrived(1, down)

            @pl.when(d == z)
            def _():
                s = jnp.where(z == n - 2, groups - 1 - t, t) if late > 0 else t
                second = (n - 1 - z) * groups + s + lag * (z - 1) <= j

                @pl.when(second)
                def _():
                    settle(t, value, jnp.logical_or(z != n - 2, t < groups - late))

                @pl.when(jnp.logical_not(second))
                def _():
                    part[d, t] = value

            extra = jnp.logical_and(z == 1, down < groups + late) if late > 0 else False

            @pl.when(jnp.logical_or(d != z, extra))
            def _():
                send(1, down, z - 1, value)

    @pl.when(middle)
    def _():
        pl.loop(0, steps - late)(pass_on)

    @pl.when(end)
    def _():
        @pl.loop(0, groups + late)
        def _(k):
            way = jnp.where(first, 1, 0)
            t = jnp.where(k < groups, k, 2 * groups - 1 - k)
            d = jnp.where(k < groups, z, jnp.where(first, 1, n - 2))
            value = part[d, t] + arrived(way, k)
            count_squares(value)

            @pl.when(k < groups)
            def _():
                rows, columns = spot(t)
                averages[:, rows, columns] = value

        if n > 2:
            pl.semaphore_wait(complete, 1)

    sums = jnp.sum(jnp.sum(squares[...], axis=1), axis=1, keepdims=True)
    lanes = norms.shape[1]
    row = lax.broadcasted_iota(jnp.int32, (widths, lanes), 0)
    col = lax.broadcasted_iota(jnp.int32, (widths, lanes), 1)
    line = jnp.sum(jnp.where(row == col, sums, 0.0), axis=0, keepdims=True)

    mine = z * peers + me
    lines[mine] = line

    def others(act):
        for p in range(n):
            def body(k, p=p):
                @pl.when(jnp.logical_or(p != z, k != me))
                def _():
                    act(p, k)

            each(peers, body)

    def line_copy(p, k, slot):
        return pltpu.make_async_remote_copy(
            src_ref=lines.at[slot], dst_ref=lines.at[slot],
            send_sem=line_send.at[p * peers + k], recv_sem=line_recv.at[slot],
            device_id={"snap": p, "param": k}, device_id_type=MESH,
        )

    others(lambda p, k: line_copy(p, k, mine).start())

    if late > 0:
        @pl.when(middle)
        def _():
            pl.loop(steps - late, steps)(pass_on)

    up_sends = (n - 1 - z) * groups
    down_sends = z * groups
    if late > 0:
        up_sends += jnp.where(z == n - 2, late, 0)
        down_sends += jnp.where(z == 1, late, 0)

    @pl.loop(0, steps)
    def _(k):
        @pl.when(k < up_sends)
        def _():
            for copy in copies(0, k, jnp.where(final, z - 1, z + 1)):
                copy.wait_send()

        @pl.when(k < down_sends)
        def _():
            for copy in copies(1, k, jnp.where(first, z + 1, z - 1)):
                copy.wait_send()

    others(lambda p, k: line_copy(p, k, mine).wait_send())
    others(lambda p, k: line_copy(p, k, p * peers + k).wait_recv())
    norms[...] = jnp.sqrt(jnp.sum(lines[...], axis=0) / jnp.float32(entries))


def on_device(n, peers, snapshots, coeffs):
    count, height, cols = snapshots.shape
    widths = coeffs.shape[0]
    keep = cols // n
    groups = height // GROUP * (keep // WIDE)
    steps = (n - 1) * groups
    entries = height * cols * peers
    dma = pltpu.SemaphoreType.DMA
    regular = pltpu.SemaphoreType.REGULAR
    averages, norms = pl.pallas_call(
        functools.partial(kernel, n, peers, entries),
        out_shape=(
            jax.ShapeDtypeStruct((widths, height, keep), jnp.float32),
            jax.ShapeDtypeStruct((1, 128), jnp.float32),
        ),
        in_specs=[pl.BlockSpec(memory_space=pltpu.HBM), pl.BlockSpec(memory_space=pl.ANY)],
        out_specs=(pl.BlockSpec(memory_space=pltpu.VMEM), pl.BlockSpec(memory_space=pltpu.VMEM)),
        scratch_shapes=[
            pltpu.VMEM((widths, count), jnp.float32),
            pltpu.VMEM((2 * widths * GROUP, count * GROUP), jnp.bfloat16),
            pltpu.VMEM((n * groups, count, GROUP, WIDE), jnp.bfloat16),
            pltpu.VMEM((n, groups, widths, GROUP, WIDE), jnp.float32),
            pltpu.VMEM((2, steps, widths, GROUP, WIDE), jnp.bfloat16),
            pltpu.VMEM((2, steps, 1, WIDE), jnp.float32),
            pltpu.VMEM((2, steps, widths, GROUP, WIDE), jnp.bfloat16),
            pltpu.VMEM((2, steps, 1, WIDE), jnp.float32),
            pltpu.VMEM((widths, 8, WIDE), jnp.float32),
            pltpu.VMEM((n * peers, 1, 128), jnp.float32),
            dma, dma((n * groups,)),
            dma((2, steps)), dma((2, steps)), dma((2, steps)), dma((2, steps)),
            dma((n * peers,)), dma((n * peers,)), regular, regular, regular, regular,
        ],
        compiler_params=pltpu.CompilerParams(
            collective_id=0, has_side_effects=True, vmem_limit_bytes=48 * 1024 * 1024
        ),
        name="reconstruct",
    )(coeffs, snapshots)
    return averages, norms[0, :widths]


def solution(mesh):
    in_specs = (P("snap", "param", None), P(None, "snap"))
    out_specs = (P(None, "param", "snap"), P())
    body = functools.partial(on_device, mesh.shape["snap"], mesh.shape["param"])
    return jax.shard_map(body, mesh=mesh, in_specs=in_specs, out_specs=out_specs, check_vma=False)
```

time: 50.4 us -> 54.3 us (1.077)
  Pallas kernels: 47.4 us -> 51.3 us
    pallas_call x1, Pallas kernels: 47.4 us -> 51.3 us  [on_device(): pl.pallas_call(functools.partial(kernel, n, peers, entries), out_shape=(j...]
where the time goes in v1:
time: 54.3 us; the launch traced here: 54.1 us
  Pallas kernels  51.3 us (94%)
  local copies, waits for them, and re-layouts  2.17 us (4%)
  between operations  0.65 us (1%)
    pallas_call x1, Pallas kernels, on_device(): pl.pallas_call(functools.partial(kernel, n, peers, entries), out_shape=(j...  51.3 us
    unnamed x3, local copies, waits for them, and re-layouts  1.66 us

profile of v1, /device:TPU:0, one launch (start us, length us, event | category | flops | bytes accessed | tf_op | source)
XLA Modules:
  0.0 54.1 jit_solution(13759780650900965966)
XLA Ops:
  0.6 0.0 copy-start
  0.6 0.7 %copy-done = f32[16,64]{1,0:T(8,128)S(1)} copy-done((f32[16,64]{1,0:T(8,128)S(1)}, f32[16,64]{1,0:T(8,128)}, u32[]{:S(2)}) %copy-start) | copy-done | bytes 4120
  1.3 51.3 %reconstruct.1 = (f32[16,64,256]{2,1,0:T(8,128)S(1)}, f32[1,128]{1,0:T(1,128)S(1)}) custom-call(f32[16,64]{1,0:T(8,128)S(1)} %copy-done, bf16[64,64,1024]{2,1,0:T(8,128)(2,1)} %stored.1), custom_call_target="tpu_custom_call" | custom-call | tf_op jit(solution)/shard_map/reconstruct/pallas_call | solution.py:384
  52.6 0.5 slice_bitcast_fusion
  53.2 1.0 %copy.5 = f32[16,64,256]{2,1,0:T(8,128)} copy(f32[16,64,256]{2,1,0:T(8,128)S(1)} %get-tuple-element.8) | data formatting | bytes 2097152
Async XLA Ops:
  0.6 0.7 %copy-start = (f32[16,64]{1,0:T(8,128)S(1)}, f32[16,64]{1,0:T(8,128)}, u32[]{:S(2)}) copy-start(f32[16,64]{1,0:T(8,128)} %coeffs.1) | copy-start | bytes 12292

commit v2 on v1

v2 whole, which is shorter than its diff:
```python
import functools

import jax
import jax.numpy as jnp
from jax import lax
from jax.experimental import pallas as pl
from jax.experimental.pallas import tpu as pltpu
from jax.sharding import PartitionSpec as P

MESH = pl.DeviceIdType.MESH
GROUP = 16
WIDE = 128
LAG = 3
LATE = 5
HOLD_FIRST = 3
HOLD_FINAL = 5
HEAD = 6
POWER = 15
AHEAD = 2
TOP = 2.0**8.375


def encode(value):
    largest = jnp.max(jnp.max(jnp.abs(value), axis=0), axis=0, keepdims=True)
    largest = jnp.maximum(largest, 1e-30)
    x = value * (TOP / largest)[None]
    x2 = x * x
    x4 = x2 * x2
    x8 = x4 * x4
    return ((x8 * x4) * (x2 * x)).astype(jnp.bfloat16), largest * (1.0 / TOP)


def decode(code, scale):
    y = code.astype(jnp.float32)
    size = jnp.exp2(jnp.log2(jnp.maximum(jnp.abs(y), 1e-38)) * (1.0 / POWER)) * scale[None]
    return jnp.where(y > 0.0, size, jnp.where(y < 0.0, -size, 0.0))


def each(size, body):
    if size <= 8:
        for k in range(size):
            body(k)
    else:
        pl.loop(0, size)(body)


def shape_of(n, height, keep):
    cuts = keep // WIDE
    groups = height // GROUP * cuts
    lag = min(LAG, groups - 1)
    late = max(0, min(LATE, groups - lag, (n - 3) * (groups - lag)))
    return cuts, groups, (n - 1) * groups, lag, late


def kernel(
    n, peers, entries, coeffs, stored, averages, norms,
    weights, spread, tiles, part, out_code, out_scale, in_code, in_scale, squares, lines, result, both_sizes,
    coeff_sem, load_sem, write_sem, hand_sem, send_sem, send_scale_sem, recv_sem, line_send, line_recv,
    known, token_up, token_down, complete,
):
    z = lax.axis_index("snap")
    me = lax.axis_index("param")
    widths, count = coeffs.shape
    keep = stored.shape[2] // n
    cuts, groups, steps, lag, late = shape_of(n, stored.shape[1], keep)
    total = n * groups // cuts
    ring = load_sem.shape[0]
    low = z < n // 2
    first, final = z == 0, z == n - 1
    end = jnp.logical_or(first, final)
    middle = jnp.logical_not(end)
    hub = middle if n > 2 else end
    head = min(HEAD, total)

    def turned(d, s, last):
        return jnp.where(d == last, groups - 1 - s, s) if late > 0 else s

    def upwards(k):
        d = n - 1 - k // groups
        return d, turned(d, lax.rem(k, groups), n - 2)

    def downwards(k):
        d = k // groups
        return d, turned(d, lax.rem(k, groups), 1)

    def own(i):
        mixed = jnp.where(end, i, i // 2) if n % 2 == 0 else i
        rising = jnp.where(end, low, lax.rem(i, 2) == 0) if n % 2 == 0 else low
        du, tu = upwards(mixed * cuts)
        dd, td = downwards(mixed * cuts)
        return jnp.where(rising, du, dd), jnp.where(rising, tu, td)

    def load(i):
        d, t = own(i)
        return pltpu.make_async_copy(
            stored.at[:, pl.ds(pl.multiple_of(t // cuts * GROUP, GROUP), GROUP), pl.ds(pl.multiple_of(d * keep, keep), keep)],
            tiles.at[i],
            load_sem.at[lax.rem(i, ring)],
        )

    load(0).start()
    read = pltpu.make_async_copy(coeffs, weights, coeff_sem)
    read.start()
    barrier = pltpu.get_barrier_semaphore()

    @pl.when(z > 0)
    def _():
        pl.semaphore_signal(barrier, inc=1, device_id={"snap": z - 1}, device_id_type=MESH)

    @pl.when(z < n - 1)
    def _():
        pl.semaphore_signal(barrier, inc=1, device_id={"snap": z + 1}, device_id_type=MESH)

    def to_peers(semaphore):
        def body(k):
            @pl.when(k != me)
            def _():
                pl.semaphore_signal(semaphore, inc=1, device_id={"param": k}, device_id_type=MESH)

        each(peers, body)

    @pl.when(hub)
    def _():
        to_peers(barrier)

    tall, wide = spread.shape
    row = lax.broadcasted_iota(jnp.int32, (count, wide), 0)
    col = lax.broadcasted_iota(jnp.int32, (count, wide), 1)
    repeat = jnp.where(col // GROUP == row, 1.0, 0.0).astype(jnp.bfloat16)
    row = lax.broadcasted_iota(jnp.int32, (GROUP, wide), 0)
    col = lax.broadcasted_iota(jnp.int32, (GROUP, wide), 1)
    same = (row == col % GROUP)[None]
    read.wait()
    whole = weights[...]
    high = whole.astype(jnp.bfloat16)
    rest = (whole - high.astype(jnp.float32)).astype(jnp.bfloat16)
    both = jnp.concatenate([high, rest], axis=0)
    full = jnp.dot(both, repeat, preferred_element_type=jnp.float32)
    full = jnp.where(same, full[:, None, :], 0.0)
    spread[...] = full.reshape(tall, wide).astype(jnp.bfloat16)
    squares[...] = jnp.zeros_like(squares)

    def copies(way, k, peer):
        code = pltpu.make_async_remote_copy(
            src_ref=out_code.at[way, k], dst_ref=in_code.at[way, k],
            send_sem=send_sem.at[way], recv_sem=recv_sem.at[way, k],
            device_id={"snap": peer}, device_id_type=MESH,
        )
        scale = pltpu.make_async_remote_copy(
            src_ref=out_scale.at[way, k], dst_ref=in_scale.at[way, k],
            send_sem=send_scale_sem.at[way], recv_sem=recv_sem.at[way, k],
            device_id={"snap": peer}, device_id_type=MESH,
        )
        return scale, code

    def launch(way, k, peer):
        for copy in copies(way, k, peer):
            copy.start()

    def pack(way, k, value):
        code, scale = encode(value)
        out_code[way, k] = code
        out_scale[way, k] = scale

    def send(way, k, peer, value):
        pack(way, k, value)
        launch(way, k, peer)

    def arrived(way, k):
        pltpu.make_async_copy(both_sizes, both_sizes, recv_sem.at[way, k]).wait()
        return decode(in_code[way, k], in_scale[way, k])

    def count_squares(value):
        squares[...] += jnp.sum((value * value).reshape(widths, GROUP // 8, 8, WIDE), axis=1)

    half = widths * GROUP

    def multiply(i):
        d, t = own(i)
        load(i).wait()

        @pl.when(i + AHEAD < total)
        def _():
            load(i + AHEAD).start()

        both_parts = jnp.dot(
            spread[...], tiles[i].reshape(count * GROUP, keep), preferred_element_type=jnp.float32
        )
        value = (both_parts[:half] + both_parts[half:]).reshape(widths, GROUP, keep)
        pieces = [value[:, :, c * WIDE:(c + 1) * WIDE] for c in range(cuts)]
        for c, piece in enumerate(pieces):
            part[d, t // cuts * cuts + c] = piece
        return d, t, pieces

    for i in range(1, min(AHEAD, total)):
        load(i).start()

    ends_way = jnp.where(first, 0, 1)
    ends_peer = jnp.where(first, 1, n - 2)
    if late > 0:
        held = steps - jnp.where(first, HOLD_FIRST, HOLD_FINAL)
    else:
        held = steps

    @pl.when(end)
    def _():
        @pl.loop(0, total)
        def _(i):
            d, t, pieces = multiply(i)

            @pl.when(i == 0)
            def _():
                pl.semaphore_wait(barrier, 1 if n > 2 else peers)

            @pl.when(d != z)
            def _():
                back = lax.rem(t, cuts) > 0
                for c, piece in enumerate(pieces):
                    k = i * cuts + jnp.where(back, cuts - 1 - c, c)
                    pack(ends_way, k, piece)

                    @pl.when(k < held)
                    def _():
                        launch(ends_way, k, ends_peer)

        if n == 2:
            to_peers(known)
            pl.semaphore_wait(known, peers - 1)

    def write(t):
        rows = pl.ds(pl.multiple_of(t // cuts * GROUP, GROUP), GROUP)
        columns = pl.ds(pl.multiple_of(lax.rem(t, cuts) * WIDE, WIDE), WIDE)
        return pltpu.make_async_copy(part.at[z, t], averages.at[:, rows, columns], write_sem)

    def settle(t, value):
        part[z, t] = value
        write(t).start()

    def both_ways(t, value, second, counted):
        @pl.when(second)
        def _():
            settle(t, value)

            @pl.when(counted)
            def _():
                count_squares(value)

        @pl.when(jnp.logical_not(second))
        def _():
            part[z, t] = value

    def pass_on(j):
        up = j - lag * (z - 1)
        down = j - lag * (n - 2 - z)

        @pl.when(jnp.logical_and(up >= 0, up < (n - z) * groups))
        def _():
            d, t = upwards(up)
            value = part[d, t] + arrived(0, up)

            @pl.when(d == z)
            def _():
                s = turned(z, t, 1)
                second = z * groups + s + lag * (n - 2 - z) < j
                both_ways(t, value, second, jnp.logical_or(z != 1, t < groups - late))

            extra = jnp.logical_and(z == n - 2, up < groups + late) if late > 0 else False

            @pl.when(jnp.logical_or(d != z, extra))
            def _():
                send(0, up, z + 1, value)

        @pl.when(jnp.logical_and(down >= 0, down < (z + 1) * groups))
        def _():
            d, t = downwards(down)
            value = part[d, t] + arrived(1, down)

            @pl.when(d == z)
            def _():
                s = turned(z, t, n - 2)
                second = (n - 1 - z) * groups + s + lag * (z - 1) <= j
                both_ways(t, value, second, jnp.logical_or(z != n - 2, t < groups - late))

            extra = jnp.logical_and(z == 1, down < groups + late) if late > 0 else False

            @pl.when(jnp.logical_or(d != z, extra))
            def _():
                send(1, down, z - 1, value)

    @pl.when(middle)
    def _():
        pl.loop(0, head)(lambda i: multiply(i) and None)
        pl.semaphore_wait(barrier, 2 + peers - 1)
        to_peers(known)

        @pl.loop(0, steps - late)
        def _(j):
            pass_on(j)

            @pl.when(j + head < total)
            def _():
                multiply(j + head)

            @pl.when(j == 2)
            def _():
                pl.semaphore_wait(known, peers - 1)

                @pl.when(z > 1)
                def _():
                    pl.semaphore_signal(token_down, inc=1, device_id={"snap": z - 1}, device_id_type=MESH)

                @pl.when(z < n - 2)
                def _():
                    pl.semaphore_signal(token_up, inc=1, device_id={"snap": z + 1}, device_id_type=MESH)

            @pl.when(j == 4)
            def _():
                @pl.when(z > 1)
                def _():
                    pl.semaphore_wait(token_up, 1)

                @pl.when(z < n - 2)
                def _():
                    pl.semaphore_wait(token_down, 1)

                @pl.when(z == 1)
                def _():
                    pl.semaphore_signal(complete, inc=1, device_id={"snap": z - 1}, device_id_type=MESH)

                @pl.when(z == n - 2)
                def _():
                    pl.semaphore_signal(complete, inc=1, device_id={"snap": z + 1}, device_id_type=MESH)

    @pl.when(end)
    def _():
        @pl.loop(0, groups + late)
        def _(k):
            t = jnp.where(k < groups, k, 2 * groups - 1 - k)
            d = jnp.where(k < groups, z, ends_peer)
            value = part[d, t] + arrived(1 - ends_way, k)
            count_squares(value)

            @pl.when(k < groups)
            def _():
                settle(t, value)

        if n > 2:
            pl.semaphore_wait(complete, 1)

    sums = jnp.sum(jnp.sum(squares[...], axis=1), axis=1, keepdims=True)
    lanes = norms.shape[1]
    row = lax.broadcasted_iota(jnp.int32, (widths, lanes), 0)
    col = lax.broadcasted_iota(jnp.int32, (widths, lanes), 1)
    line = jnp.sum(jnp.where(row == col, sums, 0.0), axis=0, keepdims=True)

    mine = z * peers + me
    lines[mine] = line

    for p in range(n):
        def body(k, p=p):
            @pl.when(jnp.logical_or(p != z, k != me))
            def _():
                pltpu.make_async_remote_copy(
                    src_ref=lines.at[mine], dst_ref=lines.at[mine], send_sem=line_send, recv_sem=line_recv,
                    device_id={"snap": p, "param": k}, device_id_type=MESH,
                ).start()

        each(peers, body)

    if late > 0:
        @pl.when(end)
        def _():
            pl.loop(held, steps)(lambda k: launch(ends_way, k, ends_peer))

        @pl.when(middle)
        def _():
            pl.loop(steps - late, steps - 1)(pass_on)

    def sent(way, amount):
        if amount > 0:
            some = pl.ds(0, amount)
            pltpu.make_async_copy(out_code.at[way, some], out_code.at[way, some], send_sem.at[way]).wait()
            pltpu.make_async_copy(out_scale.at[way, some], out_scale.at[way, some], send_scale_sem.at[way]).wait()

    def all_sent(layers):
        for layer in layers:
            @pl.when(z == layer)
            def _(layer=layer):
                sent(0, (n - 1 - layer) * groups + (late if layer == n - 2 else 0))
                sent(1, layer * groups + (late if layer == 1 else 0))

    all_sent(range(1, n - 1))
    rest_of = lines.at[pl.ds(0, n * peers - 1)]
    pltpu.make_async_copy(rest_of, rest_of, line_send).wait()
    pltpu.make_async_copy(rest_of, rest_of, line_recv).wait()
    result[...] = jnp.sqrt(jnp.sum(lines[...], axis=0) / jnp.float32(entries))
    hand = pltpu.make_async_copy(result, norms, hand_sem)
    hand.start()

    if late > 0:
        @pl.when(middle)
        def _():
            pass_on(steps - 1)

    all_sent((0, n - 1))
    pltpu.make_async_copy(averages, averages, write_sem).wait()
    hand.wait()


def on_device(n, peers, snapshots, coeffs):
    count, height, cols = snapshots.shape
    widths = coeffs.shape[0]
    keep = cols // n
    cuts, groups, steps, lag, late = shape_of(n, height, keep)
    total = n * groups // cuts
    entries = height * cols * peers
    dma = pltpu.SemaphoreType.DMA
    regular = pltpu.SemaphoreType.REGULAR
    averages, norms = pl.pallas_call(
        functools.partial(kernel, n, peers, entries),
        out_shape=(
            jax.ShapeDtypeStruct((widths, height, keep), jnp.float32),
            jax.ShapeDtypeStruct((1, 128), jnp.float32),
        ),
        in_specs=[pl.BlockSpec(memory_space=pl.ANY), pl.BlockSpec(memory_space=pl.ANY)],
        out_specs=(pl.BlockSpec(memory_space=pl.ANY), pl.BlockSpec(memory_space=pl.ANY)),
        scratch_shapes=[
            pltpu.VMEM((widths, count), jnp.float32),
            pltpu.VMEM((2 * widths * GROUP, count * GROUP), jnp.bfloat16),
            pltpu.VMEM((total, count, GROUP, keep), jnp.bfloat16),
            pltpu.VMEM((n, groups, widths, GROUP, WIDE), jnp.float32),
            pltpu.VMEM((2, steps, widths, GROUP, WIDE), jnp.bfloat16),
            pltpu.VMEM((2, steps, 1, WIDE), jnp.float32),
            pltpu.VMEM((2, steps, widths, GROUP, WIDE), jnp.bfloat16),
            pltpu.VMEM((2, steps, 1, WIDE), jnp.float32),
            pltpu.VMEM((widths, 8, WIDE), jnp.float32),
            pltpu.VMEM((n * peers, 1, 128), jnp.float32),
            pltpu.VMEM((1, 128), jnp.float32),
            pltpu.VMEM((widths * GROUP // 2 + 1, 1, WIDE), jnp.float32),
            dma, dma((AHEAD + 1,)), dma, dma, dma((2,)), dma((2,)), dma((2, steps)), dma, dma,
            regular, regular, regular, regular,
        ],
        compiler_params=pltpu.CompilerParams(
            collective_id=0, has_side_effects=True, vmem_limit_bytes=48 * 1024 * 1024
        ),
        name="reconstruct",
    )(coeffs, snapshots)
    return averages, norms[0, :widths]


def solution(mesh):
    in_specs = (P("snap", "param", None), P(None, "snap"))
    out_specs = (P(None, "param", "snap"), P())
    body = functools.partial(on_device, mesh.shape["snap"], mesh.shape["param"])
    return jax.shard_map(body, mesh=mesh, in_specs=in_specs, out_specs=out_specs, check_vma=False)
```

time: 54.3 us -> 42.7 us (0.79)
  Pallas kernels: 51.3 us -> 39.7 us
    pallas_call x1, Pallas kernels: 51.3 us -> 39.7 us  [on_device(): pl.pallas_call(functools.partial(kernel, n, peers, entries), out_shape=(j...]
where the time goes in v2:
time: 42.7 us; the launch traced here: 42.5 us
  Pallas kernels  39.7 us (93%)
  local copies, waits for them, and re-layouts  2.17 us (5%)
  between operations  0.65 us (2%)
    pallas_call x1, Pallas kernels, on_device(): pl.pallas_call(functools.partial(kernel, n, peers, entries), out_shape=(j...  39.7 us
    unnamed x3, local copies, waits for them, and re-layouts  1.66 us

profile of v2, /device:TPU:0, one launch (start us, length us, event | category | flops | bytes accessed | tf_op | source)
XLA Modules:
  0.0 42.5 jit_solution(2490049075496194807)
XLA Ops:
  0.6 0.0 copy-start
  0.6 0.7 %copy-done = f32[16,64]{1,0:T(8,128)S(1)} copy-done((f32[16,64]{1,0:T(8,128)S(1)}, f32[16,64]{1,0:T(8,128)}, u32[]{:S(2)}) %copy-start) | copy-done | bytes 4120
  1.3 39.7 %reconstruct.1 = (f32[16,64,256]{2,1,0:T(8,128)S(1)}, f32[1,128]{1,0:T(1,128)S(1)}) custom-call(f32[16,64]{1,0:T(8,128)S(1)} %copy-done, bf16[64,64,1024]{2,1,0:T(8,128)(2,1)} %stored.1), custom_call_target="tpu_custom_call" | custom-call | tf_op jit(solution)/shard_map/reconstruct/pallas_call | solution.py:419
  41.0 0.5 %slice_bitcast_fusion = f32[16]{0:T(128)} fusion(f32[1,128]{1,0:T(1,128)S(1)} %get-tuple-element.5), kind=kLoop, calls=%fused_computation | loop fusion | bytes 128 | tf_op jit(solution)/shard_map/squeeze | solution.py:448
  41.5 1.0 %copy.5 = f32[16,64,256]{2,1,0:T(8,128)} copy(f32[16,64,256]{2,1,0:T(8,128)S(1)} %get-tuple-element.8) | data formatting | bytes 2097152
Async XLA Ops:
  0.6 0.7 %copy-start = (f32[16,64]{1,0:T(8,128)S(1)}, f32[16,64]{1,0:T(8,128)}, u32[]{:S(2)}) copy-start(f32[16,64]{1,0:T(8,128)} %coeffs.1) | copy-start | bytes 12292

commit v3 on v2

--- a/solution.py
+++ b/solution.py
@@ -10,13 +10,17 @@
 MESH = pl.DeviceIdType.MESH
 GROUP = 16
 WIDE = 128
-LAG = 3
+LAG_UP = 3
+LAG_DOWN = 4
 LATE = 5
 HOLD_FIRST = 3
-HOLD_FINAL = 5
+HOLD_FINAL = 4
+KEEP_FIRST = 3
+KEEP_FINAL = 4
 HEAD = 6
 POWER = 15
 AHEAD = 2
+SPLIT = 1
 TOP = 2.0**8.375
 
 
@@ -47,9 +51,9 @@
 def shape_of(n, height, keep):
     cuts = keep // WIDE
     groups = height // GROUP * cuts
-    lag = min(LAG, groups - 1)
-    late = max(0, min(LATE, groups - lag, (n - 3) * (groups - lag)))
-    return cuts, groups, (n - 1) * groups, lag, late
+    lags = min(LAG_UP, groups - 1), min(LAG_DOWN, groups - 1)
+    late = min(LATE, groups - 1) if n > 3 else 0
+    return cuts, groups, (n - 1) * groups, lags, late
 
 
 def kernel(
@@ -62,7 +66,7 @@
     me = lax.axis_index("param")
     widths, count = coeffs.shape
     keep = stored.shape[2] // n
-    cuts, groups, steps, lag, late = shape_of(n, stored.shape[1], keep)
+    cuts, groups, steps, (lag_up, lag_down), late = shape_of(n, stored.shape[1], keep)
     total = n * groups // cuts
     ring = load_sem.shape[0]
     low = z < n // 2
@@ -71,6 +75,7 @@
     middle = jnp.logical_not(end)
     hub = middle if n > 2 else end
     head = min(HEAD, total)
+    more = max(1, 2 // cuts)
 
     def turned(d, s, last):
         return jnp.where(d == last, groups - 1 - s, s) if late > 0 else s
@@ -98,9 +103,9 @@
             load_sem.at[lax.rem(i, ring)],
         )
 
-    load(0).start()
     read = pltpu.make_async_copy(coeffs, weights, coeff_sem)
     read.start()
+    load(0).start()
     barrier = pltpu.get_barrier_semaphore()
 
     @pl.when(z > 0)
@@ -199,6 +204,7 @@
     ends_peer = jnp.where(first, 1, n - 2)
     if late > 0:
         held = steps - jnp.where(first, HOLD_FIRST, HOLD_FINAL)
+        kept = steps - jnp.where(first, KEEP_FIRST, KEEP_FINAL)
     else:
         held = steps
 
@@ -215,9 +221,9 @@
             @pl.when(d != z)
             def _():
                 back = lax.rem(t, cuts) > 0
-                for c, piece in enumerate(pieces):
-                    k = i * cuts + jnp.where(back, cuts - 1 - c, c)
-                    pack(ends_way, k, piece)
+                for c in range(cuts):
+                    k = i * cuts + c
+                    pack(ends_way, k, jnp.where(back, pieces[cuts - 1 - c], pieces[c]))
 
                     @pl.when(k < held)
                     def _():
@@ -249,10 +255,10 @@
         def _():
             part[z, t] = value
 
-    def pass_on(j):
-        up = j - lag * (z - 1)
-        down = j - lag * (n - 2 - z)
-
+    up_delay = lag_up * (z - 1)
+    down_delay = lag_down * (n - 2 - z)
+
+    def pass_up(up):
         @pl.when(jnp.logical_and(up >= 0, up < (n - z) * groups))
         def _():
             d, t = upwards(up)
@@ -261,7 +267,7 @@
             @pl.when(d == z)
             def _():
                 s = turned(z, t, 1)
-                second = z * groups + s + lag * (n - 2 - z) < j
+                second = z * groups + s + down_delay < up + up_delay
                 both_ways(t, value, second, jnp.logical_or(z != 1, t < groups - late))
 
             extra = jnp.logical_and(z == n - 2, up < groups + late) if late > 0 else False
@@ -270,6 +276,7 @@
             def _():
                 send(0, up, z + 1, value)
 
+    def pass_down(down):
         @pl.when(jnp.logical_and(down >= 0, down < (z + 1) * groups))
         def _():
             d, t = downwards(down)
@@ -278,7 +285,7 @@
             @pl.when(d == z)
             def _():
                 s = turned(z, t, n - 2)
-                second = (n - 1 - z) * groups + s + lag * (z - 1) <= j
+                second = (n - 1 - z) * groups + s + up_delay <= down + down_delay
                 both_ways(t, value, second, jnp.logical_or(z != n - 2, t < groups - late))
 
             extra = jnp.logical_and(z == 1, down < groups + late) if late > 0 else False
@@ -286,6 +293,10 @@
             @pl.when(jnp.logical_or(d != z, extra))
             def _():
                 send(1, down, z - 1, value)
+
+    def pass_on(j):
+        pass_up(j - up_delay)
+        pass_down(j - down_delay)
 
     @pl.when(middle)
     def _():
@@ -297,9 +308,10 @@
         def _(j):
             pass_on(j)
 
-            @pl.when(j + head < total)
-            def _():
-                multiply(j + head)
+            for m in range(more):
+                @pl.when(more * j + m + head < total)
+                def _(m=m):
+                    multiply(more * j + m + head)
 
             @pl.when(j == 2)
             def _():
@@ -330,11 +342,27 @@
                 @pl.when(z == n - 2)
                 def _():
                     pl.semaphore_signal(complete, inc=1, device_id={"snap": z + 1}, device_id_type=MESH)
+
+    if late > 0:
+        @pl.when(z == 1)
+        def _():
+            pl.loop(steps - late - down_delay, 2 * groups)(pass_down)
+
+        @pl.when(z == n - 2)
+        def _():
+            pl.loop(steps - late - up_delay, 2 * groups)(pass_up)
 
     @pl.when(end)
     def _():
         @pl.loop(0, groups + late)
         def _(k):
+            if late > 0:
+                early = k - (groups + late) + (kept - held)
+
+                @pl.when(early >= 0)
+                def _():
+                    launch(ends_way, held + early, ends_peer)
+
             t = jnp.where(k < groups, k, 2 * groups - 1 - k)
             d = jnp.where(k < groups, z, ends_peer)
             value = part[d, t] + arrived(1 - ends_way, k)
@@ -370,11 +398,15 @@
     if late > 0:
         @pl.when(end)
         def _():
-            pl.loop(held, steps)(lambda k: launch(ends_way, k, ends_peer))
-
-        @pl.when(middle)
-        def _():
-            pl.loop(steps - late, steps - 1)(pass_on)
+            pl.loop(kept, steps)(lambda k: launch(ends_way, k, ends_peer))
+
+        @pl.when(z == 1)
+        def _():
+            pl.loop(steps - late, steps - 1)(pass_up)
+
+        @pl.when(z == n - 2)
+        def _():
+            pl.loop(steps - late, steps - 1)(pass_down)
 
     def sent(way, amount):
         if amount > 0:
@@ -398,20 +430,56 @@
     hand.start()
 
     if late > 0:
-        @pl.when(middle)
-        def _():
-            pass_on(steps - 1)
+        @pl.when(z == 1)
+        def _():
+            pass_up(steps - 1)
+
+        @pl.when(z == n - 2)
+        def _():
+            pass_down(steps - 1)
 
     all_sent((0, n - 1))
     pltpu.make_async_copy(averages, averages, write_sem).wait()
     hand.wait()
+
+
+def hand_out(averages, norms, widths):
+    def body(averages, norms, averages_out, norms_out, line, row, sems):
+        parts = SPLIT
+        size = averages.shape[0] // parts
+
+
+        for k in range(parts):
+            some = pl.ds(k * size, size)
+            pltpu.make_async_copy(averages.at[some], averages_out.at[some], sems.at[k]).start()
+
+        row[...] = norms[0, :widths]
+        write = pltpu.make_async_copy(row, norms_out, sems.at[parts])
+        write.start()
+        for k in range(parts):
+            some = pl.ds(k * size, size)
+            pltpu.make_async_copy(averages.at[some], averages_out.at[some], sems.at[k]).wait()
+        write.wait()
+
+    anywhere = pl.BlockSpec(memory_space=pl.ANY)
+    return pl.pallas_call(
+        body,
+        out_shape=(
+            jax.ShapeDtypeStruct(averages.shape, jnp.float32),
+            jax.ShapeDtypeStruct((widths,), jnp.float32),
+        ),
+        in_specs=[pl.BlockSpec(memory_space=pltpu.VMEM)] * 2,
+        out_specs=(anywhere, anywhere),
+        scratch_shapes=[pltpu.VMEM((1, 128), jnp.float32), pltpu.VMEM((widths,), jnp.float32), pltpu.SemaphoreType.DMA((SPLIT + 1,))],
+        name="hand_out",
+    )(pltpu.with_memory_space_constraint(averages, pltpu.VMEM), pltpu.with_memory_space_constraint(norms, pltpu.VMEM))
 
 
 def on_device(n, peers, snapshots, coeffs):
     count, height, cols = snapshots.shape
     widths = coeffs.shape[0]
     keep = cols // n
-    cuts, groups, steps, lag, late = shape_of(n, height, keep)
+    cuts, groups, steps, lags, late = shape_of(n, height, keep)
     total = n * groups // cuts
     entries = height * cols * peers
     dma = pltpu.SemaphoreType.DMA
@@ -444,8 +512,8 @@
             collective_id=0, has_side_effects=True, vmem_limit_bytes=48 * 1024 * 1024
         ),
         name="reconstruct",
-    )(coeffs, snapshots)
-    return averages, norms[0, :widths]
+    )(pltpu.with_memory_space_constraint(coeffs, pltpu.HBM), snapshots)
+    return hand_out(averages, norms, widths)
 
 
 def solution(mesh):

time: 42.7 us -> 41.9 us (0.981)
  local copies, waits for them, and re-layouts: 2.17 us -> 0 us
  Pallas kernels: 39.7 us -> 41 us
    unnamed x3 -> x0, local copies, waits for them, and re-layouts: 1.66 us -> none
    pallas_call x0 -> x1, Pallas kernels: none -> 0.99 us  [hand_out(): pl.pallas_call(body, out_shape=(jax.ShapeDtypeStruct(averages.shape, jnp....]
    squeeze x1 -> x0, local copies, waits for them, and re-layouts: 0.51 us -> none  [on_device(): return (averages, norms[0, :widths])]
where the time goes in v3:
time: 41.9 us; the launch traced here: 41.6 us
  Pallas kernels  41 us (98%)
  between operations  0.64 us (2%)
    pallas_call x1, Pallas kernels, on_device(): pl.pallas_call(functools.partial(kernel, n, peers, entries), out_shape=(j...  40 us
    pallas_call x1, Pallas kernels, hand_out(): pl.pallas_call(body, out_shape=(jax.ShapeDtypeStruct(averages.shape, jnp....  0.99 us

profile of v3, /device:TPU:0, one launch (start us, length us, event | category | flops | bytes accessed | tf_op | source)
XLA Modules:
  0.0 41.6 jit_solution(1657733169004595700)
XLA Ops:
  0.6 40.0 %reconstruct.1 = (f32[16,64,256]{2,1,0:T(8,128)S(1)}, f32[1,128]{1,0:T(1,128)S(1)}) custom-call(f32[16,64]{1,0:T(8,128)} %coeffs.1, bf16[64,64,1024]{2,1,0:T(8,128)(2,1)} %stored.1), custom_call_target="tpu_custom_call" | custom-call | tf_op jit(solution)/shard_map/reconstruct/pallas_call | solution.py:487
  40.6 1.0 %hand_out.1 = (f32[16,64,256]{2,1,0:T(8,128)}, f32[16]{0:T(128)}) custom-call(f32[16,64,256]{2,1,0:T(8,128)S(1)} %get-tuple-element.4.averages, f32[1,128]{1,0:T(1,128)S(1)} %get-tuple-element.5.norms), custom_call_target="tpu_custom_call" | custom-call | tf_op jit(solution)/shard_map/hand_out/pallas_call | solution.py:465

commit v4 on v3

--- a/solution.py
+++ b/solution.py
@@ -1,4 +1,5 @@
 import functools
+import math
 
 import jax
 import jax.numpy as jnp
@@ -8,26 +9,28 @@
 from jax.sharding import PartitionSpec as P
 
 MESH = pl.DeviceIdType.MESH
-GROUP = 16
-WIDE = 128
-LAG_UP = 3
-LAG_DOWN = 4
-LATE = 5
+GROUP = 8
+LAG_UP = 2
+LAG_DOWN = 3
+LATE = 6
 HOLD_FIRST = 3
 HOLD_FINAL = 4
 KEEP_FIRST = 3
 KEEP_FINAL = 4
-HEAD = 6
+HEAD = 10
 POWER = 15
-AHEAD = 2
+AHEAD = 3
 SPLIT = 1
+SPLIT_FIRST = 1
 TOP = 2.0**8.375
+LANES = 128
 
 
 def encode(value):
-    largest = jnp.max(jnp.max(jnp.abs(value), axis=0), axis=0, keepdims=True)
-    largest = jnp.maximum(largest, 1e-30)
-    x = value * (TOP / largest)[None]
+    lanes = [value[:, c:c + LANES] for c in range(0, value.shape[1], LANES)]
+    largest = functools.reduce(jnp.maximum, [jnp.abs(lane) for lane in lanes])
+    largest = jnp.maximum(jnp.max(largest, axis=0, keepdims=True), 1e-30)
+    x = value * jnp.concatenate([TOP / largest] * len(lanes), axis=1)
     x2 = x * x
     x4 = x2 * x2
     x8 = x4 * x4
@@ -36,7 +39,8 @@
 
 def decode(code, scale):
     y = code.astype(jnp.float32)
-    size = jnp.exp2(jnp.log2(jnp.maximum(jnp.abs(y), 1e-38)) * (1.0 / POWER)) * scale[None]
+    scale = jnp.concatenate([scale] * (code.shape[1] // LANES), axis=1)
+    size = jnp.exp2(jnp.log2(jnp.maximum(jnp.abs(y), 1e-38)) * (1.0 / POWER)) * scale
     return jnp.where(y > 0.0, size, jnp.where(y < 0.0, -size, 0.0))
 
 
@@ -48,12 +52,11 @@
         pl.loop(0, size)(body)
 
 
-def shape_of(n, height, keep):
-    cuts = keep // WIDE
-    groups = height // GROUP * cuts
+def shape_of(n, height):
+    groups = height // GROUP
     lags = min(LAG_UP, groups - 1), min(LAG_DOWN, groups - 1)
     late = min(LATE, groups - 1) if n > 3 else 0
-    return cuts, groups, (n - 1) * groups, lags, late
+    return groups, (n - 1) * groups, lags, late
 
 
 def kernel(
@@ -66,8 +69,8 @@
     me = lax.axis_index("param")
     widths, count = coeffs.shape
     keep = stored.shape[2] // n
-    cuts, groups, steps, (lag_up, lag_down), late = shape_of(n, stored.shape[1], keep)
-    total = n * groups // cuts
+    groups, steps, (lag_up, lag_down), late = shape_of(n, stored.shape[1])
+    total = n * groups
     ring = load_sem.shape[0]
     low = z < n // 2
     first, final = z == 0, z == n - 1
@@ -75,7 +78,7 @@
     middle = jnp.logical_not(end)
     hub = middle if n > 2 else end
     head = min(HEAD, total)
-    more = max(1, 2 // cuts)
+    more = 2
 
     def turned(d, s, last):
         return jnp.where(d == last, groups - 1 - s, s) if late > 0 else s
@@ -91,21 +94,24 @@
     def own(i):
         mixed = jnp.where(end, i, i // 2) if n % 2 == 0 else i
         rising = jnp.where(end, low, lax.rem(i, 2) == 0) if n % 2 == 0 else low
-        du, tu = upwards(mixed * cuts)
-        dd, td = downwards(mixed * cuts)
+        du, tu = upwards(mixed)
+        dd, td = downwards(mixed)
         return jnp.where(rising, du, dd), jnp.where(rising, tu, td)
 
-    def load(i):
+    def load(i, begin=0, amount=count):
         d, t = own(i)
+        some = pl.ds(begin, amount)
         return pltpu.make_async_copy(
-            stored.at[:, pl.ds(pl.multiple_of(t // cuts * GROUP, GROUP), GROUP), pl.ds(pl.multiple_of(d * keep, keep), keep)],
-            tiles.at[i],
+            stored.at[some, pl.ds(pl.multiple_of(t * GROUP, GROUP), GROUP), pl.ds(pl.multiple_of(d * keep, keep), keep)],
+            tiles.at[i, some],
             load_sem.at[lax.rem(i, ring)],
         )
 
     read = pltpu.make_async_copy(coeffs, weights, coeff_sem)
     read.start()
-    load(0).start()
+    split = math.gcd(SPLIT_FIRST, count)
+    for c in range(split):
+        load(0, c * (count // split), count // split).start()
     barrier = pltpu.get_barrier_semaphore()
 
     @pl.when(z > 0)
@@ -145,15 +151,18 @@
     spread[...] = full.reshape(tall, wide).astype(jnp.bfloat16)
     squares[...] = jnp.zeros_like(squares)
 
+    def place(layer, way, k):
+        return jnp.where(jnp.where(layer < n // 2, 0, 1) == way, k, steps + k)
+
     def copies(way, k, peer):
         code = pltpu.make_async_remote_copy(
             src_ref=out_code.at[way, k], dst_ref=in_code.at[way, k],
-            send_sem=send_sem.at[way], recv_sem=recv_sem.at[way, k],
+            send_sem=send_sem.at[way], recv_sem=recv_sem.at[place(peer, way, k)],
             device_id={"snap": peer}, device_id_type=MESH,
         )
         scale = pltpu.make_async_remote_copy(
             src_ref=out_scale.at[way, k], dst_ref=in_scale.at[way, k],
-            send_sem=send_scale_sem.at[way], recv_sem=recv_sem.at[way, k],
+            send_sem=send_scale_sem.at[way], recv_sem=recv_sem.at[place(peer, way, k)],
             device_id={"snap": peer}, device_id_type=MESH,
         )
         return scale, code
@@ -163,7 +172,7 @@
             copy.start()
 
     def pack(way, k, value):
-        code, scale = encode(value)
+        code, scale = encode(value.reshape(widths * GROUP, keep))
         out_code[way, k] = code
         out_scale[way, k] = scale
 
@@ -172,11 +181,12 @@
         launch(way, k, peer)
 
     def arrived(way, k):
-        pltpu.make_async_copy(both_sizes, both_sizes, recv_sem.at[way, k]).wait()
-        return decode(in_code[way, k], in_scale[way, k])
+        pltpu.make_async_copy(both_sizes, both_sizes, recv_sem.at[place(z, way, k)]).wait()
+        return decode(in_code[way, k], in_scale[way, k]).reshape(widths, GROUP, keep)
 
     def count_squares(value):
-        squares[...] += jnp.sum((value * value).reshape(widths, GROUP // 8, 8, WIDE), axis=1)
+        square = value * value
+        squares[...] += sum(square[:, :, c:c + LANES] for c in range(0, keep, LANES))
 
     half = widths * GROUP
 
@@ -192,10 +202,8 @@
             spread[...], tiles[i].reshape(count * GROUP, keep), preferred_element_type=jnp.float32
         )
         value = (both_parts[:half] + both_parts[half:]).reshape(widths, GROUP, keep)
-        pieces = [value[:, :, c * WIDE:(c + 1) * WIDE] for c in range(cuts)]
-        for c, piece in enumerate(pieces):
-            part[d, t // cuts * cuts + c] = piece
-        return d, t, pieces
+        part[d, t] = value
+        return d, t, value
 
     for i in range(1, min(AHEAD, total)):
         load(i).start()
@@ -212,7 +220,7 @@
     def _():
         @pl.loop(0, total)
         def _(i):
-            d, t, pieces = multiply(i)
+            d, _, value = multiply(i)
 
             @pl.when(i == 0)
             def _():
@@ -220,23 +228,19 @@
 
             @pl.when(d != z)
             def _():
-                back = lax.rem(t, cuts) > 0
-                for c in range(cuts):
-                    k = i * cuts + c
-                    pack(ends_way, k, jnp.where(back, pieces[cuts - 1 - c], pieces[c]))
-
-                    @pl.when(k < held)
-                    def _():
-                        launch(ends_way, k, ends_peer)
+                pack(ends_way, i, value)
+
+                @pl.when(i < held)
+                def _():
+                    launch(ends_way, i, ends_peer)
 
         if n == 2:
             to_peers(known)
             pl.semaphore_wait(known, peers - 1)
 
     def write(t):
-        rows = pl.ds(pl.multiple_of(t // cuts * GROUP, GROUP), GROUP)
-        columns = pl.ds(pl.multiple_of(lax.rem(t, cuts) * WIDE, WIDE), WIDE)
-        return pltpu.make_async_copy(part.at[z, t], averages.at[:, rows, columns], write_sem)
+        rows = pl.ds(pl.multiple_of(t * GROUP, GROUP), GROUP)
+        return pltpu.make_async_copy(part.at[z, t], averages.at[:, rows, :], write_sem)
 
     def settle(t, value):
         part[z, t] = value
@@ -479,8 +483,8 @@
     count, height, cols = snapshots.shape
     widths = coeffs.shape[0]
     keep = cols // n
-    cuts, groups, steps, lags, late = shape_of(n, height, keep)
-    total = n * groups // cuts
+    groups, steps, _, _ = shape_of(n, height)
+    total = n * groups
     entries = height * cols * peers
     dma = pltpu.SemaphoreType.DMA
     regular = pltpu.SemaphoreType.REGULAR
@@ -488,7 +492,7 @@
         functools.partial(kernel, n, peers, entries),
         out_shape=(
             jax.ShapeDtypeStruct((widths, height, keep), jnp.float32),
-            jax.ShapeDtypeStruct((1, 128), jnp.float32),
+            jax.ShapeDtypeStruct((1, LANES), jnp.float32),
         ),
         in_specs=[pl.BlockSpec(memory_space=pl.ANY), pl.BlockSpec(memory_space=pl.ANY)],
         out_specs=(pl.BlockSpec(memory_space=pl.ANY), pl.BlockSpec(memory_space=pl.ANY)),
@@ -496,16 +500,16 @@
             pltpu.VMEM((widths, count), jnp.float32),
             pltpu.VMEM((2 * widths * GROUP, count * GROUP), jnp.bfloat16),
             pltpu.VMEM((total, count, GROUP, keep), jnp.bfloat16),
-            pltpu.VMEM((n, groups, widths, GROUP, WIDE), jnp.float32),
-            pltpu.VMEM((2, steps, widths, GROUP, WIDE), jnp.bfloat16),
-            pltpu.VMEM((2, steps, 1, WIDE), jnp.float32),
-            pltpu.VMEM((2, steps, widths, GROUP, WIDE), jnp.bfloat16),
-            pltpu.VMEM((2, steps, 1, WIDE), jnp.float32),
-            pltpu.VMEM((widths, 8, WIDE), jnp.float32),
-            pltpu.VMEM((n * peers, 1, 128), jnp.float32),
-            pltpu.VMEM((1, 128), jnp.float32),
-            pltpu.VMEM((widths * GROUP // 2 + 1, 1, WIDE), jnp.float32),
-            dma, dma((AHEAD + 1,)), dma, dma, dma((2,)), dma((2,)), dma((2, steps)), dma, dma,
+            pltpu.VMEM((n, groups, widths, GROUP, keep), jnp.float32),
+            pltpu.VMEM((2, steps, widths * GROUP, keep), jnp.bfloat16),
+            pltpu.VMEM((2, steps, 1, LANES), jnp.float32),
+            pltpu.VMEM((2, steps, widths * GROUP, keep), jnp.bfloat16),
+            pltpu.VMEM((2, steps, 1, LANES), jnp.float32),
+            pltpu.VMEM((widths, GROUP, LANES), jnp.float32),
+            pltpu.VMEM((n * peers, 1, LANES), jnp.float32),
+            pltpu.VMEM((1, LANES), jnp.float32),
+            pltpu.VMEM((widths * GROUP // 2 * keep // LANES + 1, 1, LANES), jnp.float32),
+            dma, dma((AHEAD + 1,)), dma, dma, dma((2,)), dma((2,)), dma((steps + max(2, n // 2) * groups,)), dma, dma,
             regular, regular, regular, regular,
         ],
         compiler_params=pltpu.CompilerParams(

time: 41.9 us -> 41 us (0.979)
  Pallas kernels: 41 us -> 40.1 us
    pallas_call x1, Pallas kernels: 40 us -> 39.1 us  [on_device(): pl.pallas_call(functools.partial(kernel, n, peers, entries), out_shape=(j...]
where the time goes in v4:
time: 41 us; the launch traced here: 40.7 us
  Pallas kernels  40.1 us (98%)
  between operations  0.64 us (2%)
    pallas_call x1, Pallas kernels, on_device(): pl.pallas_call(functools.partial(kernel, n, peers, entries), out_shape=(j...  39.1 us
    pallas_call x1, Pallas kernels, hand_out(): pl.pallas_call(body, out_shape=(jax.ShapeDtypeStruct(averages.shape, jnp....  0.99 us

profile of v4, /device:TPU:0, one launch (start us, length us, event | category | flops | bytes accessed | tf_op | source)
XLA Modules:
  0.0 40.7 jit_solution(10630408589321817786)
XLA Ops:
  0.6 39.1 %reconstruct.1 = (f32[16,64,256]{2,1,0:T(8,128)S(1)}, f32[1,128]{1,0:T(1,128)S(1)}) custom-call(f32[16,64]{1,0:T(8,128)} %coeffs.1, bf16[64,64,1024]{2,1,0:T(8,128)(2,1)} %stored.1), custom_call_target="tpu_custom_call" | custom-call | tf_op jit(solution)/shard_map/reconstruct/pallas_call | solution.py:491
  39.7 1.0 %hand_out.1 = (f32[16,64,256]{2,1,0:T(8,128)}, f32[16]{0:T(128)}) custom-call(f32[16,64,256]{2,1,0:T(8,128)S(1)} %get-tuple-element.4.averages, f32[1,128]{1,0:T(1,128)S(1)} %get-tuple-element.5.norms), custom_call_target="tpu_custom_call" | custom-call | tf_op jit(solution)/shard_map/hand_out/pallas_call | solution.py:469

commit v5 on v4

--- a/solution.py
+++ b/solution.py
@@ -13,10 +13,9 @@
 LAG_UP = 2
 LAG_DOWN = 3
 LATE = 6
-HOLD_FIRST = 3
-HOLD_FINAL = 4
-KEEP_FIRST = 3
-KEEP_FINAL = 4
+HOLD_FIRST = (3, 3)
+HOLD_FINAL = (4, 4)
+BEHIND = 3
 HEAD = 10
 POWER = 15
 AHEAD = 3
@@ -211,10 +210,14 @@
     ends_way = jnp.where(first, 0, 1)
     ends_peer = jnp.where(first, 1, n - 2)
     if late > 0:
-        held = steps - jnp.where(first, HOLD_FIRST, HOLD_FINAL)
-        kept = steps - jnp.where(first, KEEP_FIRST, KEEP_FINAL)
+        second = lax.rem(me, 2) == 1
+        held = steps - jnp.where(
+            first, jnp.where(second, HOLD_FIRST[1], HOLD_FIRST[0]), jnp.where(second, HOLD_FINAL[1], HOLD_FINAL[0])
+        )
     else:
         held = steps
+
+    behind = jnp.where(lax.rem(me, 2) == 1, BEHIND, 0)
 
     @pl.when(end)
     def _():
@@ -230,9 +233,11 @@
             def _():
                 pack(ends_way, i, value)
 
-                @pl.when(i < held)
-                def _():
-                    launch(ends_way, i, ends_peer)
+            ready = jnp.where(i == 0, 0, i - behind)
+
+            @pl.when(jnp.logical_and(jnp.logical_or(i == 0, ready > 0), ready < held))
+            def _():
+                launch(ends_way, ready, ends_peer)
 
         if n == 2:
             to_peers(known)
@@ -321,23 +326,31 @@
             def _():
                 pl.semaphore_wait(known, peers - 1)
 
+                @pl.when(jnp.logical_and(z == n - 2, z > 1))
+                def _():
+                    pl.semaphore_signal(token_down, inc=1, device_id={"snap": z - 1}, device_id_type=MESH)
+
+                @pl.when(jnp.logical_and(z == 1, z < n - 2))
+                def _():
+                    pl.semaphore_signal(token_up, inc=1, device_id={"snap": z + 1}, device_id_type=MESH)
+
+            @pl.when(j == 4)
+            def _():
                 @pl.when(z > 1)
                 def _():
+                    pl.semaphore_wait(token_up, 1)
+
+                @pl.when(jnp.logical_and(z > 1, z < n - 2))
+                def _():
+                    pl.semaphore_signal(token_up, inc=1, device_id={"snap": z + 1}, device_id_type=MESH)
+
+                @pl.when(z < n - 2)
+                def _():
+                    pl.semaphore_wait(token_down, 1)
+
+                @pl.when(jnp.logical_and(z > 1, z < n - 2))
+                def _():
                     pl.semaphore_signal(token_down, inc=1, device_id={"snap": z - 1}, device_id_type=MESH)
-
-                @pl.when(z < n - 2)
-                def _():
-                    pl.semaphore_signal(token_up, inc=1, device_id={"snap": z + 1}, device_id_type=MESH)
-
-            @pl.when(j == 4)
-            def _():
-                @pl.when(z > 1)
-                def _():
-                    pl.semaphore_wait(token_up, 1)
-
-                @pl.when(z < n - 2)
-                def _():
-                    pl.semaphore_wait(token_down, 1)
 
                 @pl.when(z == 1)
                 def _():
@@ -360,13 +373,6 @@
     def _():
         @pl.loop(0, groups + late)
         def _(k):
-            if late > 0:
-                early = k - (groups + late) + (kept - held)
-
-                @pl.when(early >= 0)
-                def _():
-                    launch(ends_way, held + early, ends_peer)
-
             t = jnp.where(k < groups, k, 2 * groups - 1 - k)
             d = jnp.where(k < groups, z, ends_peer)
             value = part[d, t] + arrived(1 - ends_way, k)
@@ -402,7 +408,7 @@
     if late > 0:
         @pl.when(end)
         def _():
-            pl.loop(kept, steps)(lambda k: launch(ends_way, k, ends_peer))
+            pl.loop(held, steps)(lambda k: launch(ends_way, k, ends_peer))
 
         @pl.when(z == 1)
         def _():

time: 41 us -> 40.5 us (0.988)
  Pallas kernels: 40.1 us -> 39.5 us
    pallas_call x1, Pallas kernels: 39.1 us -> 38.5 us  [on_device(): pl.pallas_call(functools.partial(kernel, n, peers, entries), out_shape=(j...]
where the time goes in v5:
time: 40.5 us; the launch traced here: 40.1 us
  Pallas kernels  39.5 us (98%)
  between operations  0.64 us (2%)
    pallas_call x1, Pallas kernels, on_device(): pl.pallas_call(functools.partial(kernel, n, peers, entries), out_shape=(j...  38.5 us
    pallas_call x1, Pallas kernels, hand_out(): pl.pallas_call(body, out_shape=(jax.ShapeDtypeStruct(averages.shape, jnp....  0.99 us

profile of v5, /device:TPU:0, one launch (start us, length us, event | category | flops | bytes accessed | tf_op | source)
XLA Modules:
  0.0 40.1 jit_solution(6873055884265497309)
XLA Ops:
  0.6 38.5 %reconstruct.1 = (f32[16,64,256]{2,1,0:T(8,128)S(1)}, f32[1,128]{1,0:T(1,128)S(1)}) custom-call(f32[16,64]{1,0:T(8,128)} %coeffs.1, bf16[64,64,1024]{2,1,0:T(8,128)(2,1)} %stored.1), custom_call_target="tpu_custom_call" | custom-call | tf_op jit(solution)/shard_map/reconstruct/pallas_call | solution.py:497
  39.1 1.0 %hand_out.1 = (f32[16,64,256]{2,1,0:T(8,128)}, f32[16]{0:T(128)}) custom-call(f32[16,64,256]{2,1,0:T(8,128)S(1)} %get-tuple-element.4.averages, f32[1,128]{1,0:T(1,128)S(1)} %get-tuple-element.5.norms), custom_call_target="tpu_custom_call" | custom-call | tf_op jit(solution)/shard_map/hand_out/pallas_call | solution.py:475

commit v6 on v5

--- a/solution.py
+++ b/solution.py
@@ -15,7 +15,7 @@
 LATE = 6
 HOLD_FIRST = (3, 3)
 HOLD_FINAL = (4, 4)
-BEHIND = 3
+BEHIND = (5, 3)
 HEAD = 10
 POWER = 15
 AHEAD = 3
@@ -60,8 +60,8 @@
 
 def kernel(
     n, peers, entries, coeffs, stored, averages, norms,
-    weights, spread, tiles, part, out_code, out_scale, in_code, in_scale, squares, lines, result, both_sizes,
-    coeff_sem, load_sem, write_sem, hand_sem, send_sem, send_scale_sem, recv_sem, line_send, line_recv,
+    weights, spread, tiles, part, out_code, out_scale, in_code, in_scale, squares, lines, result, sizes,
+    coeff_sem, load_sem, write_sem, send_sem, recv_sem, line_recv,
     known, token_up, token_down, complete,
 ):
     z = lax.axis_index("snap")
@@ -156,12 +156,12 @@
     def copies(way, k, peer):
         code = pltpu.make_async_remote_copy(
             src_ref=out_code.at[way, k], dst_ref=in_code.at[way, k],
-            send_sem=send_sem.at[way], recv_sem=recv_sem.at[place(peer, way, k)],
+            send_sem=send_sem, recv_sem=recv_sem.at[place(peer, way, k)],
             device_id={"snap": peer}, device_id_type=MESH,
         )
         scale = pltpu.make_async_remote_copy(
             src_ref=out_scale.at[way, k], dst_ref=in_scale.at[way, k],
-            send_sem=send_scale_sem.at[way], recv_sem=recv_sem.at[place(peer, way, k)],
+            send_sem=send_sem, recv_sem=recv_sem.at[place(peer, way, k)],
             device_id={"snap": peer}, device_id_type=MESH,
         )
         return scale, code
@@ -179,8 +179,14 @@
         pack(way, k, value)
         launch(way, k, peer)
 
+    chunk = widths * GROUP // 2 * keep // LANES + 1
+
+    def await_sizes(chunks, more_lines, semaphore):
+        some = sizes.at[pl.ds(0, chunks * chunk + more_lines)]
+        pltpu.make_async_copy(some, some, semaphore).wait()
+
     def arrived(way, k):
-        pltpu.make_async_copy(both_sizes, both_sizes, recv_sem.at[place(z, way, k)]).wait()
+        await_sizes(1, 0, recv_sem.at[place(z, way, k)])
         return decode(in_code[way, k], in_scale[way, k]).reshape(widths, GROUP, keep)
 
     def count_squares(value):
@@ -217,7 +223,7 @@
     else:
         held = steps
 
-    behind = jnp.where(lax.rem(me, 2) == 1, BEHIND, 0)
+    behind = jnp.where(lax.rem(me, 2) == 1, jnp.where(first, BEHIND[0], BEHIND[1]), 0)
 
     @pl.when(end)
     def _():
@@ -399,7 +405,7 @@
             @pl.when(jnp.logical_or(p != z, k != me))
             def _():
                 pltpu.make_async_remote_copy(
-                    src_ref=lines.at[mine], dst_ref=lines.at[mine], send_sem=line_send, recv_sem=line_recv,
+                    src_ref=lines.at[mine], dst_ref=lines.at[mine], send_sem=send_sem, recv_sem=line_recv,
                     device_id={"snap": p, "param": k}, device_id_type=MESH,
                 ).start()
 
@@ -417,26 +423,18 @@
         @pl.when(z == n - 2)
         def _():
             pl.loop(steps - late, steps - 1)(pass_down)
-
-    def sent(way, amount):
-        if amount > 0:
-            some = pl.ds(0, amount)
-            pltpu.make_async_copy(out_code.at[way, some], out_code.at[way, some], send_sem.at[way]).wait()
-            pltpu.make_async_copy(out_scale.at[way, some], out_scale.at[way, some], send_scale_sem.at[way]).wait()
 
     def all_sent(layers):
         for layer in layers:
             @pl.when(z == layer)
             def _(layer=layer):
-                sent(0, (n - 1 - layer) * groups + (late if layer == n - 2 else 0))
-                sent(1, layer * groups + (late if layer == 1 else 0))
+                extra = late * (layer == n - 2) + late * (layer == 1)
+                await_sizes((n - 1) * groups + extra, n * peers - 1, send_sem)
 
     all_sent(range(1, n - 1))
-    rest_of = lines.at[pl.ds(0, n * peers - 1)]
-    pltpu.make_async_copy(rest_of, rest_of, line_send).wait()
-    pltpu.make_async_copy(rest_of, rest_of, line_recv).wait()
+    await_sizes(0, n * peers - 1, line_recv)
     result[...] = jnp.sqrt(jnp.sum(lines[...], axis=0) / jnp.float32(entries))
-    hand = pltpu.make_async_copy(result, norms, hand_sem)
+    hand = pltpu.make_async_copy(result, norms, coeff_sem)
     hand.start()
 
     if late > 0:
@@ -514,8 +512,8 @@
             pltpu.VMEM((widths, GROUP, LANES), jnp.float32),
             pltpu.VMEM((n * peers, 1, LANES), jnp.float32),
             pltpu.VMEM((1, LANES), jnp.float32),
-            pltpu.VMEM((widths * GROUP // 2 * keep // LANES + 1, 1, LANES), jnp.float32),
-            dma, dma((AHEAD + 1,)), dma, dma, dma((2,)), dma((2,)), dma((steps + max(2, n // 2) * groups,)), dma, dma,
+            pltpu.VMEM((2 * steps * (widths * GROUP // 2 * keep // LANES + 1) + n * peers, 1, LANES), jnp.float32),
+            dma, dma((AHEAD + 1,)), dma, dma, dma((steps + max(2, n // 2) * groups,)), dma,
             regular, regular, regular, regular,
         ],
         compiler_params=pltpu.CompilerParams(

time: 40.5 us -> 40.7 us (level)
  no operation moved by 1% of the time
where the time goes in v6:
time: 40.7 us; the launch traced here: 39.9 us
  Pallas kernels  39.3 us (97%)
  between operations  0.64 us (2%)
    pallas_call x1, Pallas kernels, on_device(): pl.pallas_call(functools.partial(kernel, n, peers, entries), out_shape=(j...  38.3 us
    pallas_call x1, Pallas kernels, hand_out(): pl.pallas_call(body, out_shape=(jax.ShapeDtypeStruct(averages.shape, jnp....  0.99 us

profile of v6, /device:TPU:0, one launch (start us, length us, event | category | flops | bytes accessed | tf_op | source)
XLA Modules:
  0.0 39.9 jit_solution(11539541749631801590)
XLA Ops:
  0.6 38.3 %reconstruct.1 = (f32[16,64,256]{2,1,0:T(8,128)S(1)}, f32[1,128]{1,0:T(1,128)S(1)}) custom-call(f32[16,64]{1,0:T(8,128)} %coeffs.1, bf16[64,64,1024]{2,1,0:T(8,128)(2,1)} %stored.1), custom_call_target="tpu_custom_call" | custom-call | tf_op jit(solution)/shard_map/reconstruct/pallas_call | solution.py:495
  38.9 1.0 %hand_out.1 = (f32[16,64,256]{2,1,0:T(8,128)}, f32[16]{0:T(128)}) custom-call(f32[16,64,256]{2,1,0:T(8,128)S(1)} %get-tuple-element.4.averages, f32[1,128]{1,0:T(1,128)S(1)} %get-tuple-element.5.norms), custom_call_target="tpu_custom_call" | custom-call | tf_op jit(solution)/shard_map/hand_out/pallas_call | solution.py:473

commit v7 on v6

--- a/solution.py
+++ b/solution.py
@@ -170,6 +170,32 @@
         for copy in copies(way, k, peer):
             copy.start()
 
+    paired = late > 3 and late % 2 == 0 and n == 4
+    def in_pair(k, odd):
+        k = k - (steps - late)
+        return jnp.logical_and(jnp.logical_and(k >= 0, k < late - 2), lax.rem(k, 2) == odd)
+
+    def launch_paired(way, k, peer):
+        if not paired:
+            launch(way, k, peer)
+            return
+        leading = jnp.logical_and(final, in_pair(k, 0))
+        closing = jnp.logical_and(final, in_pair(k, 1))
+
+        @pl.when(jnp.logical_not(jnp.logical_or(leading, closing)))
+        def _():
+            launch(way, k, peer)
+
+        @pl.when(closing)
+        def _():
+            two = pl.ds(k - 1, 2)
+            for out, into in ((out_scale, in_scale), (out_code, in_code)):
+                pltpu.make_async_remote_copy(
+                    src_ref=out.at[way, two], dst_ref=into.at[way, two],
+                    send_sem=send_sem, recv_sem=recv_sem.at[place(peer, way, k - 1)],
+                    device_id={"snap": peer}, device_id_type=MESH,
+                ).start()
+
     def pack(way, k, value):
         code, scale = encode(value.reshape(widths * GROUP, keep))
         out_code[way, k] = code
@@ -186,7 +212,20 @@
         pltpu.make_async_copy(some, some, semaphore).wait()
 
     def arrived(way, k):
-        await_sizes(1, 0, recv_sem.at[place(z, way, k)])
+        if paired and isinstance(way, int) and way == 1:
+            leading = jnp.logical_and(z == n - 2, in_pair(k, 0))
+            closing = jnp.logical_and(z == n - 2, in_pair(k, 1))
+
+            @pl.when(leading)
+            def _():
+                await_sizes(2, 0, recv_sem.at[place(z, way, k)])
+
+            @pl.when(jnp.logical_not(jnp.logical_or(leading, closing)))
+            def _():
+                await_sizes(1, 0, recv_sem.at[place(z, way, k)])
+        else:
+            await_sizes(1, 0, recv_sem.at[place(z, way, k)])
+
         return decode(in_code[way, k], in_scale[way, k]).reshape(widths, GROUP, keep)
 
     def count_squares(value):
@@ -243,7 +282,7 @@
 
             @pl.when(jnp.logical_and(jnp.logical_or(i == 0, ready > 0), ready < held))
             def _():
-                launch(ends_way, ready, ends_peer)
+                launch_paired(ends_way, ready, ends_peer)
 
         if n == 2:
             to_peers(known)
@@ -414,7 +453,7 @@
     if late > 0:
         @pl.when(end)
         def _():
-            pl.loop(held, steps)(lambda k: launch(ends_way, k, ends_peer))
+            pl.loop(held, steps)(lambda k: launch_paired(ends_way, k, ends_peer))
 
         @pl.when(z == 1)
         def _():

time: 40.7 us -> 40.6 us (level)
  no operation moved by 1% of the time
where the time goes in v7:
time: 40.6 us; the launch traced here: 40 us
  Pallas kernels  39.4 us (97%)
  between operations  0.64 us (2%)
    pallas_call x1, Pallas kernels, on_device(): pl.pallas_call(functools.partial(kernel, n, peers, entries), out_shape=(j...  38.4 us
    pallas_call x1, Pallas kernels, hand_out(): pl.pallas_call(body, out_shape=(jax.ShapeDtypeStruct(averages.shape, jnp....  0.99 us

profile of v7, /device:TPU:0, one launch (start us, length us, event | category | flops | bytes accessed | tf_op | source)
XLA Modules:
  0.0 40.0 jit_solution(9393282930934095046)
XLA Ops:
  0.6 38.4 %reconstruct.1 = (f32[16,64,256]{2,1,0:T(8,128)S(1)}, f32[1,128]{1,0:T(1,128)S(1)}) custom-call(f32[16,64]{1,0:T(8,128)} %coeffs.1, bf16[64,64,1024]{2,1,0:T(8,128)(2,1)} %stored.1), custom_call_target="tpu_custom_call" | custom-call | tf_op jit(solution)/shard_map/reconstruct/pallas_call | solution.py:534
  39.0 1.0 %hand_out.1 = (f32[16,64,256]{2,1,0:T(8,128)}, f32[16]{0:T(128)}) custom-call(f32[16,64,256]{2,1,0:T(8,128)S(1)} %get-tuple-element.4.averages, f32[1,128]{1,0:T(1,128)S(1)} %get-tuple-element.5.norms), custom_call_target="tpu_custom_call" | custom-call | tf_op jit(solution)/shard_map/hand_out/pallas_call | solution.py:512
